TPU v7x, 256 devices: a whole 4x4x8 slice. The times are simulated.
256 devices in a mesh: section: 16 (over x, y), tensor: 16 (over z, core).
Axes of the slice: x: 4, y: 4, z: 8, core: 2. Of those that a mesh axis runs over, the one named last changes fastest.
Arguments:
- token_ids: int32 [3, 48], replicated, may hold values from 0 to 31999
- emb_table: bfloat16 [32000, 4096], P('section', 'tensor'), may hold values from -6 to 6
- attn_gain: bfloat16 [16, 4096], P('section'), may hold values from 0.25 to 1.75
- query_weight: bfloat16 [16, 4096, 4096], P('section', None, 'tensor'), may hold values from -8 to 8
- key_weight: bfloat16 [16, 4096, 4096], P('section', None, 'tensor'), may hold values from -8 to 8
- value_weight: bfloat16 [16, 4096, 4096], P('section', None, 'tensor'), may hold values from -0.09375 to 0.09375
- mix_weight: float32 [16, 32], P('section', 'tensor'), may hold values from 0.2 to 0.8
- out_weight: bfloat16 [16, 4096, 4096], P('section', 'tensor'), may hold values from -0.125 to 0.125
Outputs:
- layer_outputs: bfloat16 [16, 3, 48, 4096], P('section', None, None, 'tensor')
All inputs are finite; a program needn't handle non-finite values.
Results may differ from a plain program's by a relative error of at most 0.033.
Values may be sent and summed in bfloat16 or wider, within the bound.
No kernel may reach another device: no remote copies, remote signals or barrier semaphores. Data moves between devices by JAX's collectives and lax.ppermute only.
A program may use at most 64 MiB of HBM per device.

v0:
```python
import jax
import jax.numpy as jnp
from jax import lax
from jax.sharding import PartitionSpec as P

EPSILON = 1e-05
ROTARY_BASE = 10000.0


def from_everyone(array, axis):
    peers = lax.axis_size(axis)
    return lax.all_to_all(
        jnp.broadcast_to(array[None], (peers, *array.shape)), axis, 0, 0, tiled=True
    )


def of_everyone(array, axis):
    return from_everyone(array, axis).astype(jnp.float32).sum(axis=0)


def broadcast(array, axis, root):
    return lax.dynamic_index_in_dim(lax.all_gather(array, axis), root, 0, keepdims=False)


def laid_out(pieces, dim):
    lengths = list(pieces.shape[1:])
    lengths[dim] *= pieces.shape[0]
    return jnp.moveaxis(pieces, 0, dim).reshape(lengths)


def gather_directly(array, axis, dim):
    return laid_out(from_everyone(array, axis), dim)


def in_blocks(array, dim, peers):
    lengths = array.shape
    pieces = array.reshape(*lengths[:dim], peers, lengths[dim] // peers, *lengths[dim + 1 :])
    return jnp.moveaxis(pieces, dim, 0)


def summed_on_arrival(array, axis, dim):
    pieces = in_blocks(array, dim, lax.axis_size(axis))
    arrived = lax.all_to_all(pieces, axis, split_axis=0, concat_axis=0, tiled=True)
    return arrived.astype(jnp.float32).sum(axis=0)


def shifted(value, axis, steps):
    count = lax.axis_size(axis)
    first, last = (max(0, -steps), min(count, count - steps))
    return lax.ppermute(value, axis, [(source, source + steps) for source in range(first, last)])


def rms_scale(values, norm_gain):
    mean_square = jnp.mean(values * values, axis=-1, keepdims=True)
    return values * lax.rsqrt(mean_square + EPSILON) * norm_gain


def rotate(values):
    length = values.shape[-3]
    head_dim = values.shape[-1]
    half_dim = head_dim // 2
    positions = jnp.arange(length, dtype=jnp.float32)
    frequency = ROTARY_BASE ** (-(jnp.arange(half_dim, dtype=jnp.float32) * 2.0) / head_dim)
    angles = positions[:, None] * frequency[None, :]
    cosine = jnp.cos(angles)[:, None, :]
    sine_table = jnp.sin(angles)[:, None, :]
    leading = values[..., :half_dim]
    second = values[..., half_dim:]
    return jnp.concatenate(
        [leading * cosine - second * sine_table, second * cosine + leading * sine_table], axis=-1
    )


def attend(queries, key_rows, mixed_values):
    length = queries.shape[0]
    head_dim = queries.shape[2]
    scores = jnp.einsum(
        "qhd,khd->hqk", queries, key_rows, preferred_element_type=jnp.float32
    ) * head_dim ** (-0.5)
    causal = jnp.arange(length)[:, None] >= jnp.arange(length)[None, :]
    scores = jnp.where(causal, scores, -1e30)
    row_top = jnp.max(scores, axis=-1, keepdims=True)
    expo = jnp.exp(scores - row_top)
    attn_probs = (expo / jnp.sum(expo, axis=-1, keepdims=True)).astype(jnp.bfloat16)
    attended = jnp.einsum(
        "hqk,khd->qhd", attn_probs, mixed_values, preferred_element_type=jnp.float32
    )
    return attended.astype(jnp.bfloat16)


def shards(
    token_ids, emb_table, attn_gain, query_weight, key_weight, value_weight, mix_weight, out_weight
):
    section_rank = lax.axis_index("section")
    section_count = lax.axis_size("section")
    batches, length = token_ids.shape
    vocab_local, width_local = emb_table.shape
    head_local = mix_weight.shape[1]
    head_dim = query_weight.shape[2] // head_local
    norm_gain = attn_gain[0].astype(jnp.float32)
    w_query = query_weight[0]
    w_key = key_weight[0]
    w_value = value_weight[0]
    w_out = out_weight[0]
    mix_rate = mix_weight[0][None, :, None]
    flat_ids = token_ids.reshape(-1) - section_rank * vocab_local
    one_hot = (flat_ids[:, None] == jnp.arange(vocab_local, dtype=jnp.int32)[None, :]).astype(
        jnp.bfloat16
    )
    looked = jnp.dot(one_hot, emb_table, preferred_element_type=jnp.float32)
    first_shard = (
        of_everyone(looked.astype(jnp.bfloat16), "section").astype(jnp.float32).astype(jnp.bfloat16)
    )
    first_full = lax.all_gather(first_shard, "tensor", axis=1, tiled=True)
    first_float = first_full.astype(jnp.float32)

    def root_project():
        first_norm = rms_scale(first_float, norm_gain).astype(jnp.bfloat16)
        return jnp.dot(first_norm, w_value, preferred_element_type=jnp.float32).astype(jnp.bfloat16)

    def skipped():
        return jnp.zeros((first_full.shape[0], w_value.shape[1]), jnp.bfloat16)

    own_values = lax.cond(section_rank == 0, root_project, skipped)
    first_values = broadcast(own_values, "section", 0)
    source_values = first_values.reshape(batches, length, head_local, head_dim)
    first_blocks = first_shard.reshape(batches, length, width_local)

    def attention_branch(full_rows, micro_index):
        normed = rms_scale(full_rows.astype(jnp.float32), norm_gain).astype(jnp.bfloat16)
        queries = jnp.dot(normed, w_query, preferred_element_type=jnp.float32)
        key_rows = jnp.dot(normed, w_key, preferred_element_type=jnp.float32)
        values = jnp.dot(normed, w_value, preferred_element_type=jnp.float32)
        queries = rotate(queries.reshape(length, head_local, head_dim)).astype(jnp.bfloat16)
        key_rows = rotate(key_rows.reshape(length, head_local, head_dim)).astype(jnp.bfloat16)
        values = values.reshape(length, head_local, head_dim)
        picked = lax.dynamic_index_in_dim(source_values, micro_index, 0, keepdims=False).astype(
            jnp.float32
        )
        mixed_values = (mix_rate * values + (1.0 - mix_rate) * picked).astype(jnp.bfloat16)
        attended = attend(queries, key_rows, mixed_values).reshape(length, head_local * head_dim)
        return jnp.dot(attended, w_out, preferred_element_type=jnp.float32)

    def advance(step_index, loop_state):
        incoming, outputs = loop_state
        position = step_index - section_rank
        is_valid = (position >= 0) & (position < batches)
        micro_index = jnp.clip(position, 0, batches - 1)
        starting = lax.dynamic_index_in_dim(first_blocks, micro_index, 0, keepdims=False)
        shard_rows = jnp.where(section_rank == 0, starting, incoming)
        full_rows = gather_directly(shard_rows, "tensor", 1)
        summed = summed_on_arrival(
            attention_branch(full_rows, micro_index).astype(jnp.bfloat16), "tensor", 1
        )
        fresh_rows = (shard_rows.astype(jnp.float32) + summed).astype(jnp.bfloat16)
        previous = lax.dynamic_index_in_dim(outputs, micro_index, 0, keepdims=False)
        kept_rows = jnp.where(is_valid, fresh_rows, previous)
        outputs = lax.dynamic_update_index_in_dim(outputs, kept_rows, micro_index, 0)
        incoming = shifted(fresh_rows, "section", 1)
        return (incoming, outputs)

    incoming = jnp.zeros((length, width_local), jnp.bfloat16)
    outputs = jnp.zeros((batches, length, width_local), jnp.bfloat16)
    step_count = batches + section_count - 1
    incoming, outputs = lax.fori_loop(0, step_count, advance, (incoming, outputs))
    return outputs[None]


def solution(mesh):
    in_specs = (
        P(),
        P("section", "tensor"),
        P("section", None),
        P("section", None, "tensor"),
        P("section", None, "tensor"),
        P("section", None, "tensor"),
        P("section", "tensor"),
        P("section", "tensor", None),
    )
    out_specs = P("section", None, None, "tensor")
    return jax.shard_map(shards, mesh=mesh, in_specs=in_specs, out_specs=out_specs, check_vma=False)
```

profile of v0, /device:TPU:3, one launch (start us, length us, event | category | flops | bytes accessed | tf_op | source)
XLA Modules:
  0.0 1204.4 jit_solution(4408953827602636049)
XLA Ops:
  8.2 23.0 %all_to_all.29 = bf16[16,144,256]{2,1,0:T(8,128)(2,1)} all-to-all(bf16[16,144,256]{2,1,0:T(8,128)(2,1)S(1)} %broadcast_in_dim.99), channel_id=1, replica_groups=mesh['section'=16,'tensor'=16] {'section'}, dimensions={0} | all-to-all | bytes 2359296 | tf_op jit(solution)/shard_map/all_to_all | solution.py:12
  36.4 37.1 %all-gather.4.cloned.1.call-done = bf16[144,4096]{1,0:T(8,128)(2,1)} async-done(((bf16[144,256]{1,0:T(8,128)(2,1)}), bf16[144,4096]{1,0:T(8,128)(2,1)}) %all-gather.4.cloned.1.call-update) | async-done | bytes 1179664 | tf_op jit(solution)/shard_map/all_gather | solution.py:114
  85.4 36.8 %all-gather.6.cloned.1.call-done = bf16[2304,256]{1,0:T(8,128)(2,1)} async-done(((bf16[144,256]{1,0:T(8,128)(2,1)}), bf16[2304,256]{1,0:T(8,128)(2,1)}) %all-gather.6.cloned.1.call-update) | async-done | bytes 1179664 | tf_op jit(solution)/shard_map/all_gather | solution.py:22
  124.4 1073.2 %while.17 = (s32[]{:T(128)}, bf16[48,256]{1,0:T(8,128)(2,1)S(1)}, bf16[3,48,256]{2,1,0:T(8,128)(2,1)}, pred[]{:T(512)}, s32[]{:T(128)}, /*index=5*/bf16[3,48,256...) while((s32[]{:T(128)}, bf16[48,256]{1,0:T(8,128)(2,1)S(1)}, ...), condition=%wide.wide.region_9.10_spmd, body=%wide.wide.region_4.9_spmd.sunk | while | flops 407331392 | bytes 26102732 | solution.py:165
  138.9 10.5 all-to-all-done
  168.0 12.5 %all-to-all-done.1 = bf16[16,48,256]{2,1,0:T(8,128)(2,1)S(1)} async-done(((bf16[16,48,256]{2,1,0:T(8,128)(2,1)}), bf16[16,48,256]{2,1,0:T(8,128)(2,1)S(1)}, u32[]{:S(2)}, u32[]{:S(2)}) %all-to-all-start.1) | async-done | bytes 393248 | tf_op jit(solution)/shard_map/while/body/eval_jaxpr/all_to_all | solution.py:43
  198.2 10.5 all-to-all-done
  227.4 12.5 %all-to-all-done.1 = bf16[16,48,256]{2,1,0:T(8,128)(2,1)S(1)} async-done(((bf16[16,48,256]{2,1,0:T(8,128)(2,1)}), bf16[16,48,256]{2,1,0:T(8,128)(2,1)S(1)}, u32[]{:S(2)}, u32[]{:S(2)}) %all-to-all-start.1) | async-done | bytes 393248 | tf_op jit(solution)/shard_map/while/body/eval_jaxpr/all_to_all | solution.py:43
  286.7 12.5 %all-to-all-done.1 = bf16[16,48,256]{2,1,0:T(8,128)(2,1)S(1)} async-done(((bf16[16,48,256]{2,1,0:T(8,128)(2,1)}), bf16[16,48,256]{2,1,0:T(8,128)(2,1)S(1)}, u32[]{:S(2)}, u32[]{:S(2)}) %all-to-all-start.1) | async-done | bytes 393248 | tf_op jit(solution)/shard_map/while/body/eval_jaxpr/all_to_all | solution.py:43
  316.9 10.5 all-to-all-done
  346.0 12.5 %all-to-all-done.1 = bf16[16,48,256]{2,1,0:T(8,128)(2,1)S(1)} async-done(((bf16[16,48,256]{2,1,0:T(8,128)(2,1)}), bf16[16,48,256]{2,1,0:T(8,128)(2,1)S(1)}, u32[]{:S(2)}, u32[]{:S(2)}) %all-to-all-start.1) | async-done | bytes 393248 | tf_op jit(solution)/shard_map/while/body/eval_jaxpr/all_to_all | solution.py:43
  405.4 12.5 %all-to-all-done.1 = bf16[16,48,256]{2,1,0:T(8,128)(2,1)S(1)} async-done(((bf16[16,48,256]{2,1,0:T(8,128)(2,1)}), bf16[16,48,256]{2,1,0:T(8,128)(2,1)S(1)}, u32[]{:S(2)}, u32[]{:S(2)}) %all-to-all-start.1) | async-done | bytes 393248 | tf_op jit(solution)/shard_map/while/body/eval_jaxpr/all_to_all | solution.py:43
  435.5 10.5 all-to-all-done
  464.7 12.5 %all-to-all-done.1 = bf16[16,48,256]{2,1,0:T(8,128)(2,1)S(1)} async-done(((bf16[16,48,256]{2,1,0:T(8,128)(2,1)}), bf16[16,48,256]{2,1,0:T(8,128)(2,1)S(1)}, u32[]{:S(2)}, u32[]{:S(2)}) %all-to-all-start.1) | async-done | bytes 393248 | tf_op jit(solution)/shard_map/while/body/eval_jaxpr/all_to_all | solution.py:43
  524.0 12.5 %all-to-all-done.1 = bf16[16,48,256]{2,1,0:T(8,128)(2,1)S(1)} async-done(((bf16[16,48,256]{2,1,0:T(8,128)(2,1)}), bf16[16,48,256]{2,1,0:T(8,128)(2,1)S(1)}, u32[]{:S(2)}, u32[]{:S(2)}) %all-to-all-start.1) | async-done | bytes 393248 | tf_op jit(solution)/shard_map/while/body/eval_jaxpr/all_to_all | solution.py:43
  554.2 10.5 all-to-all-done
  583.4 12.5 %all-to-all-done.1 = bf16[16,48,256]{2,1,0:T(8,128)(2,1)S(1)} async-done(((bf16[16,48,256]{2,1,0:T(8,128)(2,1)}), bf16[16,48,256]{2,1,0:T(8,128)(2,1)S(1)}, u32[]{:S(2)}, u32[]{:S(2)}) %all-to-all-start.1) | async-done | bytes 393248 | tf_op jit(solution)/shard_map/while/body/eval_jaxpr/all_to_all | solution.py:43
  642.7 12.5 %all-to-all-done.1 = bf16[16,48,256]{2,1,0:T(8,128)(2,1)S(1)} async-done(((bf16[16,48,256]{2,1,0:T(8,128)(2,1)}), bf16[16,48,256]{2,1,0:T(8,128)(2,1)S(1)}, u32[]{:S(2)}, u32[]{:S(2)}) %all-to-all-start.1) | async-done | bytes 393248 | tf_op jit(solution)/shard_map/while/body/eval_jaxpr/all_to_all | solution.py:43
  672.9 10.5 all-to-all-done
  702.0 12.5 %all-to-all-done.1 = bf16[16,48,256]{2,1,0:T(8,128)(2,1)S(1)} async-done(((bf16[16,48,256]{2,1,0:T(8,128)(2,1)}), bf16[16,48,256]{2,1,0:T(8,128)(2,1)S(1)}, u32[]{:S(2)}, u32[]{:S(2)}) %all-to-all-start.1) | async-done | bytes 393248 | tf_op jit(solution)/shard_map/while/body/eval_jaxpr/all_to_all | solution.py:43
  761.4 12.5 %all-to-all-done.1 = bf16[16,48,256]{2,1,0:T(8,128)(2,1)S(1)} async-done(((bf16[16,48,256]{2,1,0:T(8,128)(2,1)}), bf16[16,48,256]{2,1,0:T(8,128)(2,1)S(1)}, u32[]{:S(2)}, u32[]{:S(2)}) %all-to-all-start.1) | async-done | bytes 393248 | tf_op jit(solution)/shard_map/while/body/eval_jaxpr/all_to_all | solution.py:43
  791.5 10.5 all-to-all-done
  820.7 12.5 %all-to-all-done.1 = bf16[16,48,256]{2,1,0:T(8,128)(2,1)S(1)} async-done(((bf16[16,48,256]{2,1,0:T(8,128)(2,1)}), bf16[16,48,256]{2,1,0:T(8,128)(2,1)S(1)}, u32[]{:S(2)}, u32[]{:S(2)}) %all-to-all-start.1) | async-done | bytes 393248 | tf_op jit(solution)/shard_map/while/body/eval_jaxpr/all_to_all | solution.py:43
  880.0 12.5 %all-to-all-done.1 = bf16[16,48,256]{2,1,0:T(8,128)(2,1)S(1)} async-done(((bf16[16,48,256]{2,1,0:T(8,128)(2,1)}), bf16[16,48,256]{2,1,0:T(8,128)(2,1)S(1)}, u32[]{:S(2)}, u32[]{:S(2)}) %all-to-all-start.1) | async-done | bytes 393248 | tf_op jit(solution)/shard_map/while/body/eval_jaxpr/all_to_all | solution.py:43
  910.2 10.5 all-to-all-done
  939.4 12.5 %all-to-all-done.1 = bf16[16,48,256]{2,1,0:T(8,128)(2,1)S(1)} async-done(((bf16[16,48,256]{2,1,0:T(8,128)(2,1)}), bf16[16,48,256]{2,1,0:T(8,128)(2,1)S(1)}, u32[]{:S(2)}, u32[]{:S(2)}) %all-to-all-start.1) | async-done | bytes 393248 | tf_op jit(solution)/shard_map/while/body/eval_jaxpr/all_to_all | solution.py:43
  998.7 12.5 %all-to-all-done.1 = bf16[16,48,256]{2,1,0:T(8,128)(2,1)S(1)} async-done(((bf16[16,48,256]{2,1,0:T(8,128)(2,1)}), bf16[16,48,256]{2,1,0:T(8,128)(2,1)S(1)}, u32[]{:S(2)}, u32[]{:S(2)}) %all-to-all-start.1) | async-done | bytes 393248 | tf_op jit(solution)/shard_map/while/body/eval_jaxpr/all_to_all | solution.py:43
  1028.9 10.5 all-to-all-done
  1058.1 12.5 %all-to-all-done.1 = bf16[16,48,256]{2,1,0:T(8,128)(2,1)S(1)} async-done(((bf16[16,48,256]{2,1,0:T(8,128)(2,1)}), bf16[16,48,256]{2,1,0:T(8,128)(2,1)S(1)}, u32[]{:S(2)}, u32[]{:S(2)}) %all-to-all-start.1) | async-done | bytes 393248 | tf_op jit(solution)/shard_map/while/body/eval_jaxpr/all_to_all | solution.py:43
  1117.4 12.5 %all-to-all-done.1 = bf16[16,48,256]{2,1,0:T(8,128)(2,1)S(1)} async-done(((bf16[16,48,256]{2,1,0:T(8,128)(2,1)}), bf16[16,48,256]{2,1,0:T(8,128)(2,1)S(1)}, u32[]{:S(2)}, u32[]{:S(2)}) %all-to-all-start.1) | async-done | bytes 393248 | tf_op jit(solution)/shard_map/while/body/eval_jaxpr/all_to_all | solution.py:43
  1147.5 10.5 all-to-all-done
  1176.7 12.5 %all-to-all-done.1 = bf16[16,48,256]{2,1,0:T(8,128)(2,1)S(1)} async-done(((bf16[16,48,256]{2,1,0:T(8,128)(2,1)}), bf16[16,48,256]{2,1,0:T(8,128)(2,1)S(1)}, u32[]{:S(2)}, u32[]{:S(2)}) %all-to-all-start.1) | async-done | bytes 393248 | tf_op jit(solution)/shard_map/while/body/eval_jaxpr/all_to_all | solution.py:43
  (613 shorter events, 760.6 us)
Async XLA Ops:
  6.5 67.0 %all-gather.4.cloned.1.call-start = ((), (), s32[]{:S(2)}) async-start(), calls=%async_computation.3 | async-start | bytes 1253376 | tf_op jit(solution)/shard_map/all_gather | solution.py:114
  33.4 88.8 %all-gather.6.cloned.1.call-start = ((), (), s32[]{:S(2)}) async-start(), calls=%async_computation.4 | async-start | bytes 1253376 | tf_op jit(solution)/shard_map/all_gather | solution.py:22
  125.9 23.5 %all-to-all-start = ((bf16[16,48,256]{2,1,0:T(8,128)(2,1)}), bf16[16,48,256]{2,1,0:T(8,128)(2,1)S(1)}, u32[]{:S(2)}, u32[]{:S(2)}) async-start(bf16[16,48,256]{2,1,0:T(8,128)(2,1)} %broadcast_in_dim.123), calls=%async_computation | async-start | bytes 786432 | tf_op jit(solution)/shard_map/while/body/eval_jaxpr/all_to_all | solution.py:12
  190.4 18.3 %all-to-all-start = ((bf16[16,48,256]{2,1,0:T(8,128)(2,1)}), bf16[16,48,256]{2,1,0:T(8,128)(2,1)S(1)}, u32[]{:S(2)}, u32[]{:S(2)}) async-start(bf16[16,48,256]{2,1,0:T(8,128)(2,1)} %broadcast_in_dim.123), calls=%async_computation | async-start | bytes 786432 | tf_op jit(solution)/shard_map/while/body/eval_jaxpr/all_to_all | solution.py:12
  222.6 17.4 %all-to-all-start.1 = ((bf16[16,48,256]{2,1,0:T(8,128)(2,1)}), bf16[16,48,256]{2,1,0:T(8,128)(2,1)S(1)}, u32[]{:S(2)}, u32[]{:S(2)}) async-start(bf16[16,48,256]{2,1,0:T(8,128)(2,1)} %bitcast.132), calls=%async_computation.1 | async-start | bytes 786432 | tf_op jit(solution)/shard_map/while/body/eval_jaxpr/all_to_all | solution.py:43
  249.7 18.3 %all-to-all-start = ((bf16[16,48,256]{2,1,0:T(8,128)(2,1)}), bf16[16,48,256]{2,1,0:T(8,128)(2,1)S(1)}, u32[]{:S(2)}, u32[]{:S(2)}) async-start(bf16[16,48,256]{2,1,0:T(8,128)(2,1)} %broadcast_in_dim.123), calls=%async_computation | async-start | bytes 786432 | tf_op jit(solution)/shard_map/while/body/eval_jaxpr/all_to_all | solution.py:12
  309.1 18.3 %all-to-all-start = ((bf16[16,48,256]{2,1,0:T(8,128)(2,1)}), bf16[16,48,256]{2,1,0:T(8,128)(2,1)S(1)}, u32[]{:S(2)}, u32[]{:S(2)}) async-start(bf16[16,48,256]{2,1,0:T(8,128)(2,1)} %broadcast_in_dim.123), calls=%async_computation | async-start | bytes 786432 | tf_op jit(solution)/shard_map/while/body/eval_jaxpr/all_to_all | solution.py:12
  368.4 18.3 %all-to-all-start = ((bf16[16,48,256]{2,1,0:T(8,128)(2,1)}), bf16[16,48,256]{2,1,0:T(8,128)(2,1)S(1)}, u32[]{:S(2)}, u32[]{:S(2)}) async-start(bf16[16,48,256]{2,1,0:T(8,128)(2,1)} %broadcast_in_dim.123), calls=%async_computation | async-start | bytes 786432 | tf_op jit(solution)/shard_map/while/body/eval_jaxpr/all_to_all | solution.py:12
  400.5 17.4 %all-to-all-start.1 = ((bf16[16,48,256]{2,1,0:T(8,128)(2,1)}), bf16[16,48,256]{2,1,0:T(8,128)(2,1)S(1)}, u32[]{:S(2)}, u32[]{:S(2)}) async-start(bf16[16,48,256]{2,1,0:T(8,128)(2,1)} %bitcast.132), calls=%async_computation.1 | async-start | bytes 786432 | tf_op jit(solution)/shard_map/while/body/eval_jaxpr/all_to_all | solution.py:43
  427.8 18.3 %all-to-all-start = ((bf16[16,48,256]{2,1,0:T(8,128)(2,1)}), bf16[16,48,256]{2,1,0:T(8,128)(2,1)S(1)}, u32[]{:S(2)}, u32[]{:S(2)}) async-start(bf16[16,48,256]{2,1,0:T(8,128)(2,1)} %broadcast_in_dim.123), calls=%async_computation | async-start | bytes 786432 | tf_op jit(solution)/shard_map/while/body/eval_jaxpr/all_to_all | solution.py:12
  459.9 17.4 %all-to-all-start.1 = ((bf16[16,48,256]{2,1,0:T(8,128)(2,1)}), bf16[16,48,256]{2,1,0:T(8,128)(2,1)S(1)}, u32[]{:S(2)}, u32[]{:S(2)}) async-start(bf16[16,48,256]{2,1,0:T(8,128)(2,1)} %bitcast.132), calls=%async_computation.1 | async-start | bytes 786432 | tf_op jit(solution)/shard_map/while/body/eval_jaxpr/all_to_all | solution.py:43
  487.1 18.3 %all-to-all-start = ((bf16[16,48,256]{2,1,0:T(8,128)(2,1)}), bf16[16,48,256]{2,1,0:T(8,128)(2,1)S(1)}, u32[]{:S(2)}, u32[]{:S(2)}) async-start(bf16[16,48,256]{2,1,0:T(8,128)(2,1)} %broadcast_in_dim.123), calls=%async_computation | async-start | bytes 786432 | tf_op jit(solution)/shard_map/while/body/eval_jaxpr/all_to_all | solution.py:12
  519.2 17.4 %all-to-all-start.1 = ((bf16[16,48,256]{2,1,0:T(8,128)(2,1)}), bf16[16,48,256]{2,1,0:T(8,128)(2,1)S(1)}, u32[]{:S(2)}, u32[]{:S(2)}) async-start(bf16[16,48,256]{2,1,0:T(8,128)(2,1)} %bitcast.132), calls=%async_computation.1 | async-start | bytes 786432 | tf_op jit(solution)/shard_map/while/body/eval_jaxpr/all_to_all | solution.py:43
  546.4 18.3 %all-to-all-start = ((bf16[16,48,256]{2,1,0:T(8,128)(2,1)}), bf16[16,48,256]{2,1,0:T(8,128)(2,1)S(1)}, u32[]{:S(2)}, u32[]{:S(2)}) async-start(bf16[16,48,256]{2,1,0:T(8,128)(2,1)} %broadcast_in_dim.123), calls=%async_computation | async-start | bytes 786432 | tf_op jit(solution)/shard_map/while/body/eval_jaxpr/all_to_all | solution.py:12
  578.6 17.4 %all-to-all-start.1 = ((bf16[16,48,256]{2,1,0:T(8,128)(2,1)}), bf16[16,48,256]{2,1,0:T(8,128)(2,1)S(1)}, u32[]{:S(2)}, u32[]{:S(2)}) async-start(bf16[16,48,256]{2,1,0:T(8,128)(2,1)} %bitcast.132), calls=%async_computation.1 | async-start | bytes 786432 | tf_op jit(solution)/shard_map/while/body/eval_jaxpr/all_to_all | solution.py:43
  605.7 18.3 %all-to-all-start = ((bf16[16,48,256]{2,1,0:T(8,128)(2,1)}), bf16[16,48,256]{2,1,0:T(8,128)(2,1)S(1)}, u32[]{:S(2)}, u32[]{:S(2)}) async-start(bf16[16,48,256]{2,1,0:T(8,128)(2,1)} %broadcast_in_dim.123), calls=%async_computation | async-start | bytes 786432 | tf_op jit(solution)/shard_map/while/body/eval_jaxpr/all_to_all | solution.py:12
  637.9 17.4 %all-to-all-start.1 = ((bf16[16,48,256]{2,1,0:T(8,128)(2,1)}), bf16[16,48,256]{2,1,0:T(8,128)(2,1)S(1)}, u32[]{:S(2)}, u32[]{:S(2)}) async-start(bf16[16,48,256]{2,1,0:T(8,128)(2,1)} %bitcast.132), calls=%async_computation.1 | async-start | bytes 786432 | tf_op jit(solution)/shard_map/while/body/eval_jaxpr/all_to_all | solution.py:43
  665.1 18.3 %all-to-all-start = ((bf16[16,48,256]{2,1,0:T(8,128)(2,1)}), bf16[16,48,256]{2,1,0:T(8,128)(2,1)S(1)}, u32[]{:S(2)}, u32[]{:S(2)}) async-start(bf16[16,48,256]{2,1,0:T(8,128)(2,1)} %broadcast_in_dim.123), calls=%async_computation | async-start | bytes 786432 | tf_op jit(solution)/shard_map/while/body/eval_jaxpr/all_to_all | solution.py:12
  697.2 17.4 %all-to-all-start.1 = ((bf16[16,48,256]{2,1,0:T(8,128)(2,1)}), bf16[16,48,256]{2,1,0:T(8,128)(2,1)S(1)}, u32[]{:S(2)}, u32[]{:S(2)}) async-start(bf16[16,48,256]{2,1,0:T(8,128)(2,1)} %bitcast.132), calls=%async_computation.1 | async-start | bytes 786432 | tf_op jit(solution)/shard_map/while/body/eval_jaxpr/all_to_all | solution.py:43
  724.4 18.3 %all-to-all-start = ((bf16[16,48,256]{2,1,0:T(8,128)(2,1)}), bf16[16,48,256]{2,1,0:T(8,128)(2,1)S(1)}, u32[]{:S(2)}, u32[]{:S(2)}) async-start(bf16[16,48,256]{2,1,0:T(8,128)(2,1)} %broadcast_in_dim.123), calls=%async_computation | async-start | bytes 786432 | tf_op jit(solution)/shard_map/while/body/eval_jaxpr/all_to_all | solution.py:12
  756.6 17.4 %all-to-all-start.1 = ((bf16[16,48,256]{2,1,0:T(8,128)(2,1)}), bf16[16,48,256]{2,1,0:T(8,128)(2,1)S(1)}, u32[]{:S(2)}, u32[]{:S(2)}) async-start(bf16[16,48,256]{2,1,0:T(8,128)(2,1)} %bitcast.132), calls=%async_computation.1 | async-start | bytes 786432 | tf_op jit(solution)/shard_map/while/body/eval_jaxpr/all_to_all | solution.py:43
  783.8 18.3 %all-to-all-start = ((bf16[16,48,256]{2,1,0:T(8,128)(2,1)}), bf16[16,48,256]{2,1,0:T(8,128)(2,1)S(1)}, u32[]{:S(2)}, u32[]{:S(2)}) async-start(bf16[16,48,256]{2,1,0:T(8,128)(2,1)} %broadcast_in_dim.123), calls=%async_computation | async-start | bytes 786432 | tf_op jit(solution)/shard_map/while/body/eval_jaxpr/all_to_all | solution.py:12
  815.9 17.4 %all-to-all-start.1 = ((bf16[16,48,256]{2,1,0:T(8,128)(2,1)}), bf16[16,48,256]{2,1,0:T(8,128)(2,1)S(1)}, u32[]{:S(2)}, u32[]{:S(2)}) async-start(bf16[16,48,256]{2,1,0:T(8,128)(2,1)} %bitcast.132), calls=%async_computation.1 | async-start | bytes 786432 | tf_op jit(solution)/shard_map/while/body/eval_jaxpr/all_to_all | solution.py:43
  843.1 18.3 %all-to-all-start = ((bf16[16,48,256]{2,1,0:T(8,128)(2,1)}), bf16[16,48,256]{2,1,0:T(8,128)(2,1)S(1)}, u32[]{:S(2)}, u32[]{:S(2)}) async-start(bf16[16,48,256]{2,1,0:T(8,128)(2,1)} %broadcast_in_dim.123), calls=%async_computation | async-start | bytes 786432 | tf_op jit(solution)/shard_map/while/body/eval_jaxpr/all_to_all | solution.py:12
  875.2 17.4 %all-to-all-start.1 = ((bf16[16,48,256]{2,1,0:T(8,128)(2,1)}), bf16[16,48,256]{2,1,0:T(8,128)(2,1)S(1)}, u32[]{:S(2)}, u32[]{:S(2)}) async-start(bf16[16,48,256]{2,1,0:T(8,128)(2,1)} %bitcast.132), calls=%async_computation.1 | async-start | bytes 786432 | tf_op jit(solution)/shard_map/while/body/eval_jaxpr/all_to_all | solution.py:43
  902.4 18.3 %all-to-all-start = ((bf16[16,48,256]{2,1,0:T(8,128)(2,1)}), bf16[16,48,256]{2,1,0:T(8,128)(2,1)S(1)}, u32[]{:S(2)}, u32[]{:S(2)}) async-start(bf16[16,48,256]{2,1,0:T(8,128)(2,1)} %broadcast_in_dim.123), calls=%async_computation | async-start | bytes 786432 | tf_op jit(solution)/shard_map/while/body/eval_jaxpr/all_to_all | solution.py:12
  961.7 18.3 %all-to-all-start = ((bf16[16,48,256]{2,1,0:T(8,128)(2,1)}), bf16[16,48,256]{2,1,0:T(8,128)(2,1)S(1)}, u32[]{:S(2)}, u32[]{:S(2)}) async-start(bf16[16,48,256]{2,1,0:T(8,128)(2,1)} %broadcast_in_dim.123), calls=%async_computation | async-start | bytes 786432 | tf_op jit(solution)/shard_map/while/body/eval_jaxpr/all_to_all | solution.py:12
  993.9 17.4 %all-to-all-start.1 = ((bf16[16,48,256]{2,1,0:T(8,128)(2,1)}), bf16[16,48,256]{2,1,0:T(8,128)(2,1)S(1)}, u32[]{:S(2)}, u32[]{:S(2)}) async-start(bf16[16,48,256]{2,1,0:T(8,128)(2,1)} %bitcast.132), calls=%async_computation.1 | async-start | bytes 786432 | tf_op jit(solution)/shard_map/while/body/eval_jaxpr/all_to_all | solution.py:43
  1021.1 18.3 %all-to-all-start = ((bf16[16,48,256]{2,1,0:T(8,128)(2,1)}), bf16[16,48,256]{2,1,0:T(8,128)(2,1)S(1)}, u32[]{:S(2)}, u32[]{:S(2)}) async-start(bf16[16,48,256]{2,1,0:T(8,128)(2,1)} %broadcast_in_dim.123), calls=%async_computation | async-start | bytes 786432 | tf_op jit(solution)/shard_map/while/body/eval_jaxpr/all_to_all | solution.py:12
  1080.4 18.3 %all-to-all-start = ((bf16[16,48,256]{2,1,0:T(8,128)(2,1)}), bf16[16,48,256]{2,1,0:T(8,128)(2,1)S(1)}, u32[]{:S(2)}, u32[]{:S(2)}) async-start(bf16[16,48,256]{2,1,0:T(8,128)(2,1)} %broadcast_in_dim.123), calls=%async_computation | async-start | bytes 786432 | tf_op jit(solution)/shard_map/while/body/eval_jaxpr/all_to_all | solution.py:12
  1112.6 17.4 %all-to-all-start.1 = ((bf16[16,48,256]{2,1,0:T(8,128)(2,1)}), bf16[16,48,256]{2,1,0:T(8,128)(2,1)S(1)}, u32[]{:S(2)}, u32[]{:S(2)}) async-start(bf16[16,48,256]{2,1,0:T(8,128)(2,1)} %bitcast.132), calls=%async_computation.1 | async-start | bytes 786432 | tf_op jit(solution)/shard_map/while/body/eval_jaxpr/all_to_all | solution.py:43
  1139.8 18.3 %all-to-all-start = ((bf16[16,48,256]{2,1,0:T(8,128)(2,1)}), bf16[16,48,256]{2,1,0:T(8,128)(2,1)S(1)}, u32[]{:S(2)}, u32[]{:S(2)}) async-start(bf16[16,48,256]{2,1,0:T(8,128)(2,1)} %broadcast_in_dim.123), calls=%async_computation | async-start | bytes 786432 | tf_op jit(solution)/shard_map/while/body/eval_jaxpr/all_to_all | solution.py:12
  (82 other events, 462.8 us)
Sparse Core Ops, SparseCore 0:
  33.5 39.9 all-gather.3
  77.2 44.8 all-gather.5
where the time goes:
time: 1220 us; the launch traced here: 1200 us
  waiting for transfers between devices  579 us (47%)
  matrix products  177 us (15%)
  starting transfers between devices  171 us (14%)
  local copies, waits for them, and re-layouts  128 us (10%)
  other arithmetic  111 us (9%)
  blocking collectives  23 us (2%)
  between operations  13.5 us (1%)
    all_to_all x18, waiting for transfers between devices, summed_on_arrival(): lax.all_to_all(pieces, axis, split_axis=0, concat_axis=0, tiled=True)  226 us
    all_to_all x18, waiting for transfers between devices, from_everyone(): lax.all_to_all(jnp.broadcast_to(array[None], (peers, *array.shape)), axis...  190 us
    ppermute x18, waiting for transfers between devices, shifted(): lax.ppermute(value, axis, [(source, source + steps) for source in range(f...  89.4 us
    all_to_all x18, starting transfers between devices, from_everyone(): lax.all_to_all(jnp.broadcast_to(array[None], (peers, *array.shape)), axis...  74.2 us
    all_to_all x18, starting transfers between devices, summed_on_arrival(): lax.all_to_all(pieces, axis, split_axis=0, concat_axis=0, tiled=True)  62.1 us
    dot_general x18, matrix products, attention_branch(): key_rows = jnp.dot(normed, w_key, preferred_element_type=jnp.float32)  44.8 us
    dot_general x18, matrix products, attend(): jnp.einsum('hqk,khd->qhd', attn_probs, mixed_values, preferred_element_ty...  40.9 us
    sub x18, matrix products, attend(): expo = jnp.exp(scores - row_top)  40 us
  transfers between devices with their start and end apart: 56, of which 56 were waited for; matrix products, arithmetic and copies ran while one was open for 9% of the time, Pallas kernels for 0%

commit v1 on v0

--- a/solution.py
+++ b/solution.py
@@ -111,7 +111,9 @@
     first_shard = (
         of_everyone(looked.astype(jnp.bfloat16), "section").astype(jnp.float32).astype(jnp.bfloat16)
     )
-    first_full = lax.all_gather(first_shard, "tensor", axis=1, tiled=True)
+    arr_next = jnp.stack([first_shard for _ in range(lax.axis_size("tensor"))], 0)
+    high = lax.all_to_all(arr_next, "tensor", 0, 0)
+    first_full = jnp.concatenate(high, 1)
     first_float = first_full.astype(jnp.float32)
 
     def root_project():

time: 1220 us -> 1220 us (level)
    all_gather x1 -> x0, waiting for transfers between devices: 37.1 us -> none  [shards(): first_full = lax.all_gather(first_shard, 'tensor', axis=1, tiled=True)]
    all_to_all x0 -> x1, waiting for transfers between devices: none -> 27.7 us  [shards(): high = lax.all_to_all(arr_next, 'tensor', 0, 0)]
where the time goes in v1:
time: 1220 us; the launch traced here: 1210 us
  waiting for transfers between devices  571 us (47%)
  starting transfers between devices  181 us (15%)
  matrix products  177 us (15%)
  local copies, waits for them, and re-layouts  130 us (11%)
  other arithmetic  108 us (9%)
  blocking collectives  23 us (2%)
  between operations  13.5 us (1%)
    all_to_all x18, waiting for transfers between devices, summed_on_arrival(): lax.all_to_all(pieces, axis, split_axis=0, concat_axis=0, tiled=True)  226 us
    all_to_all x18, waiting for transfers between devices, from_everyone(): lax.all_to_all(jnp.broadcast_to(array[None], (peers, *array.shape)), axis...  190 us
    ppermute x18, waiting for transfers between devices, shifted(): lax.ppermute(value, axis, [(source, source + steps) for source in range(f...  89.4 us
    all_to_all x18, starting transfers between devices, from_everyone(): lax.all_to_all(jnp.broadcast_to(array[None], (peers, *array.shape)), axis...  74.2 us
    all_to_all x18, starting transfers between devices, summed_on_arrival(): lax.all_to_all(pieces, axis, split_axis=0, concat_axis=0, tiled=True)  62.1 us
    dot_general x18, matrix products, attention_branch(): key_rows = jnp.dot(normed, w_key, preferred_element_type=jnp.float32)  44.8 us
    dot_general x18, matrix products, attend(): jnp.einsum('hqk,khd->qhd', attn_probs, mixed_values, preferred_element_ty...  40.9 us
    sub x18, matrix products, attend(): expo = jnp.exp(scores - row_top)  39.6 us
  transfers between devices with their start and end apart: 56, of which 56 were waited for; matrix products, arithmetic and copies ran while one was open for 9% of the time, Pallas kernels for 0%

profile of v1, /device:TPU:3, one launch (start us, length us, event | category | flops | bytes accessed | tf_op | source)
XLA Modules:
  0.0 1206.3 jit_solution(8325237393521581783)
XLA Ops:
  8.2 23.0 %all_to_all.34 = bf16[16,144,256]{2,1,0:T(8,128)(2,1)} all-to-all(bf16[16,144,256]{2,1,0:T(8,128)(2,1)S(1)} %broadcast_in_dim.99), channel_id=1, replica_groups=mesh['section'=16,'tensor'=16] {'section'}, dimensions={0} | all-to-all | bytes 2359296 | tf_op jit(solution)/shard_map/all_to_all | solution.py:12
  35.3 10.6 all-to-all-start.3
  48.9 27.7 %all-to-all-done.3 = bf16[16,144,256]{2,1,0:T(8,128)(2,1)} async-done(((bf16[16,144,256]{2,1,0:T(8,128)(2,1)}), bf16[16,144,256]{2,1,0:T(8,128)(2,1)}, u32[]{:S(2)}, u32[]{:S(2)}) %all-to-all-start.3) | async-done | bytes 1179680 | tf_op jit(solution)/shard_map/all_to_all | solution.py:115
  85.6 38.1 %all-gather.3.cloned.1.call-done = bf16[2304,256]{1,0:T(8,128)(2,1)} async-done(((bf16[144,256]{1,0:T(8,128)(2,1)}), bf16[2304,256]{1,0:T(8,128)(2,1)}) %all-gather.3.cloned.1.call-update) | async-done | bytes 1179664 | tf_op jit(solution)/shard_map/all_gather | solution.py:22
  125.8 1073.7 %while.17 = (s32[]{:T(128)}, bf16[48,256]{1,0:T(8,128)(2,1)S(1)}, bf16[3,48,256]{2,1,0:T(8,128)(2,1)}, pred[]{:T(512)}, s32[]{:T(128)}, /*index=5*/bf16[3,48,256...) while((s32[]{:T(128)}, bf16[48,256]{1,0:T(8,128)(2,1)S(1)}, ...), condition=%wide.wide.region_9.10_spmd, body=%wide.wide.region_4.9_spmd.sunk | while | flops 407331392 | bytes 26102732 | solution.py:167
  169.5 12.5 %all-to-all-done.1 = bf16[16,48,256]{2,1,0:T(8,128)(2,1)S(1)} async-done(((bf16[16,48,256]{2,1,0:T(8,128)(2,1)}), bf16[16,48,256]{2,1,0:T(8,128)(2,1)S(1)}, u32[]{:S(2)}, u32[]{:S(2)}) %all-to-all-start.1) | async-done | bytes 393248 | tf_op jit(solution)/shard_map/while/body/eval_jaxpr/all_to_all | solution.py:43
  199.6 10.6 all-to-all-done
  228.8 12.5 %all-to-all-done.1 = bf16[16,48,256]{2,1,0:T(8,128)(2,1)S(1)} async-done(((bf16[16,48,256]{2,1,0:T(8,128)(2,1)}), bf16[16,48,256]{2,1,0:T(8,128)(2,1)S(1)}, u32[]{:S(2)}, u32[]{:S(2)}) %all-to-all-start.1) | async-done | bytes 393248 | tf_op jit(solution)/shard_map/while/body/eval_jaxpr/all_to_all | solution.py:43
  288.2 12.5 %all-to-all-done.1 = bf16[16,48,256]{2,1,0:T(8,128)(2,1)S(1)} async-done(((bf16[16,48,256]{2,1,0:T(8,128)(2,1)}), bf16[16,48,256]{2,1,0:T(8,128)(2,1)S(1)}, u32[]{:S(2)}, u32[]{:S(2)}) %all-to-all-start.1) | async-done | bytes 393248 | tf_op jit(solution)/shard_map/while/body/eval_jaxpr/all_to_all | solution.py:43
  318.3 10.6 all-to-all-done
  347.6 12.5 %all-to-all-done.1 = bf16[16,48,256]{2,1,0:T(8,128)(2,1)S(1)} async-done(((bf16[16,48,256]{2,1,0:T(8,128)(2,1)}), bf16[16,48,256]{2,1,0:T(8,128)(2,1)S(1)}, u32[]{:S(2)}, u32[]{:S(2)}) %all-to-all-start.1) | async-done | bytes 393248 | tf_op jit(solution)/shard_map/while/body/eval_jaxpr/all_to_all | solution.py:43
  406.9 12.5 %all-to-all-done.1 = bf16[16,48,256]{2,1,0:T(8,128)(2,1)S(1)} async-done(((bf16[16,48,256]{2,1,0:T(8,128)(2,1)}), bf16[16,48,256]{2,1,0:T(8,128)(2,1)S(1)}, u32[]{:S(2)}, u32[]{:S(2)}) %all-to-all-start.1) | async-done | bytes 393248 | tf_op jit(solution)/shard_map/while/body/eval_jaxpr/all_to_all | solution.py:43
  437.1 10.6 all-to-all-done
  466.3 12.5 %all-to-all-done.1 = bf16[16,48,256]{2,1,0:T(8,128)(2,1)S(1)} async-done(((bf16[16,48,256]{2,1,0:T(8,128)(2,1)}), bf16[16,48,256]{2,1,0:T(8,128)(2,1)S(1)}, u32[]{:S(2)}, u32[]{:S(2)}) %all-to-all-start.1) | async-done | bytes 393248 | tf_op jit(solution)/shard_map/while/body/eval_jaxpr/all_to_all | solution.py:43
  525.6 12.5 %all-to-all-done.1 = bf16[16,48,256]{2,1,0:T(8,128)(2,1)S(1)} async-done(((bf16[16,48,256]{2,1,0:T(8,128)(2,1)}), bf16[16,48,256]{2,1,0:T(8,128)(2,1)S(1)}, u32[]{:S(2)}, u32[]{:S(2)}) %all-to-all-start.1) | async-done | bytes 393248 | tf_op jit(solution)/shard_map/while/body/eval_jaxpr/all_to_all | solution.py:43
  555.8 10.6 all-to-all-done
  585.0 12.5 %all-to-all-done.1 = bf16[16,48,256]{2,1,0:T(8,128)(2,1)S(1)} async-done(((bf16[16,48,256]{2,1,0:T(8,128)(2,1)}), bf16[16,48,256]{2,1,0:T(8,128)(2,1)S(1)}, u32[]{:S(2)}, u32[]{:S(2)}) %all-to-all-start.1) | async-done | bytes 393248 | tf_op jit(solution)/shard_map/while/body/eval_jaxpr/all_to_all | solution.py:43
  644.3 12.5 %all-to-all-done.1 = bf16[16,48,256]{2,1,0:T(8,128)(2,1)S(1)} async-done(((bf16[16,48,256]{2,1,0:T(8,128)(2,1)}), bf16[16,48,256]{2,1,0:T(8,128)(2,1)S(1)}, u32[]{:S(2)}, u32[]{:S(2)}) %all-to-all-start.1) | async-done | bytes 393248 | tf_op jit(solution)/shard_map/while/body/eval_jaxpr/all_to_all | solution.py:43
  674.5 10.6 all-to-all-done
  703.7 12.5 %all-to-all-done.1 = bf16[16,48,256]{2,1,0:T(8,128)(2,1)S(1)} async-done(((bf16[16,48,256]{2,1,0:T(8,128)(2,1)}), bf16[16,48,256]{2,1,0:T(8,128)(2,1)S(1)}, u32[]{:S(2)}, u32[]{:S(2)}) %all-to-all-start.1) | async-done | bytes 393248 | tf_op jit(solution)/shard_map/while/body/eval_jaxpr/all_to_all | solution.py:43
  763.1 12.5 %all-to-all-done.1 = bf16[16,48,256]{2,1,0:T(8,128)(2,1)S(1)} async-done(((bf16[16,48,256]{2,1,0:T(8,128)(2,1)}), bf16[16,48,256]{2,1,0:T(8,128)(2,1)S(1)}, u32[]{:S(2)}, u32[]{:S(2)}) %all-to-all-start.1) | async-done | bytes 393248 | tf_op jit(solution)/shard_map/while/body/eval_jaxpr/all_to_all | solution.py:43
  793.2 10.6 all-to-all-done
  822.4 12.5 %all-to-all-done.1 = bf16[16,48,256]{2,1,0:T(8,128)(2,1)S(1)} async-done(((bf16[16,48,256]{2,1,0:T(8,128)(2,1)}), bf16[16,48,256]{2,1,0:T(8,128)(2,1)S(1)}, u32[]{:S(2)}, u32[]{:S(2)}) %all-to-all-start.1) | async-done | bytes 393248 | tf_op jit(solution)/shard_map/while/body/eval_jaxpr/all_to_all | solution.py:43
  881.8 12.5 %all-to-all-done.1 = bf16[16,48,256]{2,1,0:T(8,128)(2,1)S(1)} async-done(((bf16[16,48,256]{2,1,0:T(8,128)(2,1)}), bf16[16,48,256]{2,1,0:T(8,128)(2,1)S(1)}, u32[]{:S(2)}, u32[]{:S(2)}) %all-to-all-start.1) | async-done | bytes 393248 | tf_op jit(solution)/shard_map/while/body/eval_jaxpr/all_to_all | solution.py:43
  911.9 10.6 all-to-all-done
  941.2 12.5 %all-to-all-done.1 = bf16[16,48,256]{2,1,0:T(8,128)(2,1)S(1)} async-done(((bf16[16,48,256]{2,1,0:T(8,128)(2,1)}), bf16[16,48,256]{2,1,0:T(8,128)(2,1)S(1)}, u32[]{:S(2)}, u32[]{:S(2)}) %all-to-all-start.1) | async-done | bytes 393248 | tf_op jit(solution)/shard_map/while/body/eval_jaxpr/all_to_all | solution.py:43
  1000.5 12.5 %all-to-all-done.1 = bf16[16,48,256]{2,1,0:T(8,128)(2,1)S(1)} async-done(((bf16[16,48,256]{2,1,0:T(8,128)(2,1)}), bf16[16,48,256]{2,1,0:T(8,128)(2,1)S(1)}, u32[]{:S(2)}, u32[]{:S(2)}) %all-to-all-start.1) | async-done | bytes 393248 | tf_op jit(solution)/shard_map/while/body/eval_jaxpr/all_to_all | solution.py:43
  1030.7 10.6 all-to-all-done
  1059.9 12.5 %all-to-all-done.1 = bf16[16,48,256]{2,1,0:T(8,128)(2,1)S(1)} async-done(((bf16[16,48,256]{2,1,0:T(8,128)(2,1)}), bf16[16,48,256]{2,1,0:T(8,128)(2,1)S(1)}, u32[]{:S(2)}, u32[]{:S(2)}) %all-to-all-start.1) | async-done | bytes 393248 | tf_op jit(solution)/shard_map/while/body/eval_jaxpr/all_to_all | solution.py:43
  1119.2 12.5 %all-to-all-done.1 = bf16[16,48,256]{2,1,0:T(8,128)(2,1)S(1)} async-done(((bf16[16,48,256]{2,1,0:T(8,128)(2,1)}), bf16[16,48,256]{2,1,0:T(8,128)(2,1)S(1)}, u32[]{:S(2)}, u32[]{:S(2)}) %all-to-all-start.1) | async-done | bytes 393248 | tf_op jit(solution)/shard_map/while/body/eval_jaxpr/all_to_all | solution.py:43
  1149.4 10.6 all-to-all-done
  1178.6 12.5 %all-to-all-done.1 = bf16[16,48,256]{2,1,0:T(8,128)(2,1)S(1)} async-done(((bf16[16,48,256]{2,1,0:T(8,128)(2,1)}), bf16[16,48,256]{2,1,0:T(8,128)(2,1)S(1)}, u32[]{:S(2)}, u32[]{:S(2)}) %all-to-all-start.1) | async-done | bytes 393248 | tf_op jit(solution)/shard_map/while/body/eval_jaxpr/all_to_all | solution.py:43
  (612 shorter events, 770.2 us)
Async XLA Ops:
  35.3 41.3 %all-to-all-start.3 = ((bf16[16,144,256]{2,1,0:T(8,128)(2,1)}), bf16[16,144,256]{2,1,0:T(8,128)(2,1)}, u32[]{:S(2)}, u32[]{:S(2)}) async-start(bf16[16,144,256]{2,1,0:T(8,128)(2,1)} %stack.2), calls=%async_computation.3 | async-start | bytes 2359296 | tf_op jit(solution)/shard_map/all_to_all | solution.py:115
  45.9 77.7 %all-gather.3.cloned.1.call-start = ((), (), s32[]{:S(2)}) async-start(), calls=%async_computation.4 | async-start | bytes 1253376 | tf_op jit(solution)/shard_map/all_gather | solution.py:22
  127.3 23.5 %all-to-all-start = ((bf16[16,48,256]{2,1,0:T(8,128)(2,1)}), bf16[16,48,256]{2,1,0:T(8,128)(2,1)S(1)}, u32[]{:S(2)}, u32[]{:S(2)}) async-start(bf16[16,48,256]{2,1,0:T(8,128)(2,1)} %broadcast_in_dim.123), calls=%async_computation | async-start | bytes 786432 | tf_op jit(solution)/shard_map/while/body/eval_jaxpr/all_to_all | solution.py:12
  164.7 17.4 %all-to-all-start.1 = ((bf16[16,48,256]{2,1,0:T(8,128)(2,1)}), bf16[16,48,256]{2,1,0:T(8,128)(2,1)S(1)}, u32[]{:S(2)}, u32[]{:S(2)}) async-start(bf16[16,48,256]{2,1,0:T(8,128)(2,1)} %bitcast.135), calls=%async_computation.1 | async-start | bytes 786432 | tf_op jit(solution)/shard_map/while/body/eval_jaxpr/all_to_all | solution.py:43
  191.9 18.3 %all-to-all-start = ((bf16[16,48,256]{2,1,0:T(8,128)(2,1)}), bf16[16,48,256]{2,1,0:T(8,128)(2,1)S(1)}, u32[]{:S(2)}, u32[]{:S(2)}) async-start(bf16[16,48,256]{2,1,0:T(8,128)(2,1)} %broadcast_in_dim.123), calls=%async_computation | async-start | bytes 786432 | tf_op jit(solution)/shard_map/while/body/eval_jaxpr/all_to_all | solution.py:12
  224.0 17.4 %all-to-all-start.1 = ((bf16[16,48,256]{2,1,0:T(8,128)(2,1)}), bf16[16,48,256]{2,1,0:T(8,128)(2,1)S(1)}, u32[]{:S(2)}, u32[]{:S(2)}) async-start(bf16[16,48,256]{2,1,0:T(8,128)(2,1)} %bitcast.135), calls=%async_computation.1 | async-start | bytes 786432 | tf_op jit(solution)/shard_map/while/body/eval_jaxpr/all_to_all | solution.py:43
  251.2 18.3 %all-to-all-start = ((bf16[16,48,256]{2,1,0:T(8,128)(2,1)}), bf16[16,48,256]{2,1,0:T(8,128)(2,1)S(1)}, u32[]{:S(2)}, u32[]{:S(2)}) async-start(bf16[16,48,256]{2,1,0:T(8,128)(2,1)} %broadcast_in_dim.123), calls=%async_computation | async-start | bytes 786432 | tf_op jit(solution)/shard_map/while/body/eval_jaxpr/all_to_all | solution.py:12
  283.4 17.4 %all-to-all-start.1 = ((bf16[16,48,256]{2,1,0:T(8,128)(2,1)}), bf16[16,48,256]{2,1,0:T(8,128)(2,1)S(1)}, u32[]{:S(2)}, u32[]{:S(2)}) async-start(bf16[16,48,256]{2,1,0:T(8,128)(2,1)} %bitcast.135), calls=%async_computation.1 | async-start | bytes 786432 | tf_op jit(solution)/shard_map/while/body/eval_jaxpr/all_to_all | solution.py:43
  310.6 18.3 %all-to-all-start = ((bf16[16,48,256]{2,1,0:T(8,128)(2,1)}), bf16[16,48,256]{2,1,0:T(8,128)(2,1)S(1)}, u32[]{:S(2)}, u32[]{:S(2)}) async-start(bf16[16,48,256]{2,1,0:T(8,128)(2,1)} %broadcast_in_dim.123), calls=%async_computation | async-start | bytes 786432 | tf_op jit(solution)/shard_map/while/body/eval_jaxpr/all_to_all | solution.py:12
  342.7 17.4 %all-to-all-start.1 = ((bf16[16,48,256]{2,1,0:T(8,128)(2,1)}), bf16[16,48,256]{2,1,0:T(8,128)(2,1)S(1)}, u32[]{:S(2)}, u32[]{:S(2)}) async-start(bf16[16,48,256]{2,1,0:T(8,128)(2,1)} %bitcast.135), calls=%async_computation.1 | async-start | bytes 786432 | tf_op jit(solution)/shard_map/while/body/eval_jaxpr/all_to_all | solution.py:43
  369.9 18.3 %all-to-all-start = ((bf16[16,48,256]{2,1,0:T(8,128)(2,1)}), bf16[16,48,256]{2,1,0:T(8,128)(2,1)S(1)}, u32[]{:S(2)}, u32[]{:S(2)}) async-start(bf16[16,48,256]{2,1,0:T(8,128)(2,1)} %broadcast_in_dim.123), calls=%async_computation | async-start | bytes 786432 | tf_op jit(solution)/shard_map/while/body/eval_jaxpr/all_to_all | solution.py:12
  402.1 17.4 %all-to-all-start.1 = ((bf16[16,48,256]{2,1,0:T(8,128)(2,1)}), bf16[16,48,256]{2,1,0:T(8,128)(2,1)S(1)}, u32[]{:S(2)}, u32[]{:S(2)}) async-start(bf16[16,48,256]{2,1,0:T(8,128)(2,1)} %bitcast.135), calls=%async_computation.1 | async-start | bytes 786432 | tf_op jit(solution)/shard_map/while/body/eval_jaxpr/all_to_all | solution.py:43
  429.3 18.3 %all-to-all-start = ((bf16[16,48,256]{2,1,0:T(8,128)(2,1)}), bf16[16,48,256]{2,1,0:T(8,128)(2,1)S(1)}, u32[]{:S(2)}, u32[]{:S(2)}) async-start(bf16[16,48,256]{2,1,0:T(8,128)(2,1)} %broadcast_in_dim.123), calls=%async_computation | async-start | bytes 786432 | tf_op jit(solution)/shard_map/while/body/eval_jaxpr/all_to_all | solution.py:12
  461.5 17.4 %all-to-all-start.1 = ((bf16[16,48,256]{2,1,0:T(8,128)(2,1)}), bf16[16,48,256]{2,1,0:T(8,128)(2,1)S(1)}, u32[]{:S(2)}, u32[]{:S(2)}) async-start(bf16[16,48,256]{2,1,0:T(8,128)(2,1)} %bitcast.135), calls=%async_computation.1 | async-start | bytes 786432 | tf_op jit(solution)/shard_map/while/body/eval_jaxpr/all_to_all | solution.py:43
  488.7 18.3 %all-to-all-start = ((bf16[16,48,256]{2,1,0:T(8,128)(2,1)}), bf16[16,48,256]{2,1,0:T(8,128)(2,1)S(1)}, u32[]{:S(2)}, u32[]{:S(2)}) async-start(bf16[16,48,256]{2,1,0:T(8,128)(2,1)} %broadcast_in_dim.123), calls=%async_computation | async-start | bytes 786432 | tf_op jit(solution)/shard_map/while/body/eval_jaxpr/all_to_all | solution.py:12
  520.8 17.4 %all-to-all-start.1 = ((bf16[16,48,256]{2,1,0:T(8,128)(2,1)}), bf16[16,48,256]{2,1,0:T(8,128)(2,1)S(1)}, u32[]{:S(2)}, u32[]{:S(2)}) async-start(bf16[16,48,256]{2,1,0:T(8,128)(2,1)} %bitcast.135), calls=%async_computation.1 | async-start | bytes 786432 | tf_op jit(solution)/shard_map/while/body/eval_jaxpr/all_to_all | solution.py:43
  548.0 18.3 %all-to-all-start = ((bf16[16,48,256]{2,1,0:T(8,128)(2,1)}), bf16[16,48,256]{2,1,0:T(8,128)(2,1)S(1)}, u32[]{:S(2)}, u32[]{:S(2)}) async-start(bf16[16,48,256]{2,1,0:T(8,128)(2,1)} %broadcast_in_dim.123), calls=%async_computation | async-start | bytes 786432 | tf_op jit(solution)/shard_map/while/body/eval_jaxpr/all_to_all | solution.py:12
  607.4 18.3 %all-to-all-start = ((bf16[16,48,256]{2,1,0:T(8,128)(2,1)}), bf16[16,48,256]{2,1,0:T(8,128)(2,1)S(1)}, u32[]{:S(2)}, u32[]{:S(2)}) async-start(bf16[16,48,256]{2,1,0:T(8,128)(2,1)} %broadcast_in_dim.123), calls=%async_computation | async-start | bytes 786432 | tf_op jit(solution)/shard_map/while/body/eval_jaxpr/all_to_all | solution.py:12
  639.5 17.4 %all-to-all-start.1 = ((bf16[16,48,256]{2,1,0:T(8,128)(2,1)}), bf16[16,48,256]{2,1,0:T(8,128)(2,1)S(1)}, u32[]{:S(2)}, u32[]{:S(2)}) async-start(bf16[16,48,256]{2,1,0:T(8,128)(2,1)} %bitcast.135), calls=%async_computation.1 | async-start | bytes 786432 | tf_op jit(solution)/shard_map/while/body/eval_jaxpr/all_to_all | solution.py:43
  666.8 18.3 %all-to-all-start = ((bf16[16,48,256]{2,1,0:T(8,128)(2,1)}), bf16[16,48,256]{2,1,0:T(8,128)(2,1)S(1)}, u32[]{:S(2)}, u32[]{:S(2)}) async-start(bf16[16,48,256]{2,1,0:T(8,128)(2,1)} %broadcast_in_dim.123), calls=%async_computation | async-start | bytes 786432 | tf_op jit(solution)/shard_map/while/body/eval_jaxpr/all_to_all | solution.py:12
  726.1 18.3 %all-to-all-start = ((bf16[16,48,256]{2,1,0:T(8,128)(2,1)}), bf16[16,48,256]{2,1,0:T(8,128)(2,1)S(1)}, u32[]{:S(2)}, u32[]{:S(2)}) async-start(bf16[16,48,256]{2,1,0:T(8,128)(2,1)} %broadcast_in_dim.123), calls=%async_computation | async-start | bytes 786432 | tf_op jit(solution)/shard_map/while/body/eval_jaxpr/all_to_all | solution.py:12
  758.3 17.4 %all-to-all-start.1 = ((bf16[16,48,256]{2,1,0:T(8,128)(2,1)}), bf16[16,48,256]{2,1,0:T(8,128)(2,1)S(1)}, u32[]{:S(2)}, u32[]{:S(2)}) async-start(bf16[16,48,256]{2,1,0:T(8,128)(2,1)} %bitcast.135), calls=%async_computation.1 | async-start | bytes 786432 | tf_op jit(solution)/shard_map/while/body/eval_jaxpr/all_to_all | solution.py:43
  785.5 18.3 %all-to-all-start = ((bf16[16,48,256]{2,1,0:T(8,128)(2,1)}), bf16[16,48,256]{2,1,0:T(8,128)(2,1)S(1)}, u32[]{:S(2)}, u32[]{:S(2)}) async-start(bf16[16,48,256]{2,1,0:T(8,128)(2,1)} %broadcast_in_dim.123), calls=%async_computation | async-start | bytes 786432 | tf_op jit(solution)/shard_map/while/body/eval_jaxpr/all_to_all | solution.py:12
  844.8 18.3 %all-to-all-start = ((bf16[16,48,256]{2,1,0:T(8,128)(2,1)}), bf16[16,48,256]{2,1,0:T(8,128)(2,1)S(1)}, u32[]{:S(2)}, u32[]{:S(2)}) async-start(bf16[16,48,256]{2,1,0:T(8,128)(2,1)} %broadcast_in_dim.123), calls=%async_computation | async-start | bytes 786432 | tf_op jit(solution)/shard_map/while/body/eval_jaxpr/all_to_all | solution.py:12
  877.0 17.4 %all-to-all-start.1 = ((bf16[16,48,256]{2,1,0:T(8,128)(2,1)}), bf16[16,48,256]{2,1,0:T(8,128)(2,1)S(1)}, u32[]{:S(2)}, u32[]{:S(2)}) async-start(bf16[16,48,256]{2,1,0:T(8,128)(2,1)} %bitcast.135), calls=%async_computation.1 | async-start | bytes 786432 | tf_op jit(solution)/shard_map/while/body/eval_jaxpr/all_to_all | solution.py:43
  904.2 18.3 %all-to-all-start = ((bf16[16,48,256]{2,1,0:T(8,128)(2,1)}), bf16[16,48,256]{2,1,0:T(8,128)(2,1)S(1)}, u32[]{:S(2)}, u32[]{:S(2)}) async-start(bf16[16,48,256]{2,1,0:T(8,128)(2,1)} %broadcast_in_dim.123), calls=%async_computation | async-start | bytes 786432 | tf_op jit(solution)/shard_map/while/body/eval_jaxpr/all_to_all | solution.py:12
  963.5 18.3 %all-to-all-start = ((bf16[16,48,256]{2,1,0:T(8,128)(2,1)}), bf16[16,48,256]{2,1,0:T(8,128)(2,1)S(1)}, u32[]{:S(2)}, u32[]{:S(2)}) async-start(bf16[16,48,256]{2,1,0:T(8,128)(2,1)} %broadcast_in_dim.123), calls=%async_computation | async-start | bytes 786432 | tf_op jit(solution)/shard_map/while/body/eval_jaxpr/all_to_all | solution.py:12
  995.7 17.4 %all-to-all-start.1 = ((bf16[16,48,256]{2,1,0:T(8,128)(2,1)}), bf16[16,48,256]{2,1,0:T(8,128)(2,1)S(1)}, u32[]{:S(2)}, u32[]{:S(2)}) async-start(bf16[16,48,256]{2,1,0:T(8,128)(2,1)} %bitcast.135), calls=%async_computation.1 | async-start | bytes 786432 | tf_op jit(solution)/shard_map/while/body/eval_jaxpr/all_to_all | solution.py:43
  1022.9 18.3 %all-to-all-start = ((bf16[16,48,256]{2,1,0:T(8,128)(2,1)}), bf16[16,48,256]{2,1,0:T(8,128)(2,1)S(1)}, u32[]{:S(2)}, u32[]{:S(2)}) async-start(bf16[16,48,256]{2,1,0:T(8,128)(2,1)} %broadcast_in_dim.123), calls=%async_computation | async-start | bytes 786432 | tf_op jit(solution)/shard_map/while/body/eval_jaxpr/all_to_all | solution.py:12
  1082.3 18.3 %all-to-all-start = ((bf16[16,48,256]{2,1,0:T(8,128)(2,1)}), bf16[16,48,256]{2,1,0:T(8,128)(2,1)S(1)}, u32[]{:S(2)}, u32[]{:S(2)}) async-start(bf16[16,48,256]{2,1,0:T(8,128)(2,1)} %broadcast_in_dim.123), calls=%async_computation | async-start | bytes 786432 | tf_op jit(solution)/shard_map/while/body/eval_jaxpr/all_to_all | solution.py:12
  1114.4 17.4 %all-to-all-start.1 = ((bf16[16,48,256]{2,1,0:T(8,128)(2,1)}), bf16[16,48,256]{2,1,0:T(8,128)(2,1)S(1)}, u32[]{:S(2)}, u32[]{:S(2)}) async-start(bf16[16,48,256]{2,1,0:T(8,128)(2,1)} %bitcast.135), calls=%async_computation.1 | async-start | bytes 786432 | tf_op jit(solution)/shard_map/while/body/eval_jaxpr/all_to_all | solution.py:43
  1141.6 18.3 %all-to-all-start = ((bf16[16,48,256]{2,1,0:T(8,128)(2,1)}), bf16[16,48,256]{2,1,0:T(8,128)(2,1)S(1)}, u32[]{:S(2)}, u32[]{:S(2)}) async-start(bf16[16,48,256]{2,1,0:T(8,128)(2,1)} %broadcast_in_dim.123), calls=%async_computation | async-start | bytes 786432 | tf_op jit(solution)/shard_map/while/body/eval_jaxpr/all_to_all | solution.py:12
  (82 other events, 437.8 us)
Sparse Core Ops, SparseCore 0:
  77.4 46.1 all-gather.2
